TPU v7x, 32 devices: a whole 2x2x4 slice. The times are simulated.
32 devices in a mesh: slab: 4 (over x, core), img: 8 (over z, y).
Axes of the slice: x: 2, y: 2, z: 4, core: 2. Of those that a mesh axis runs over, the one named last changes fastest.
Arguments:
- feats: bfloat16 [8, 32, 128, 512], P('img', 'slab'), may hold values from -6 to 6
- labels: int32 [8], P('img'), may hold values from 0 to 999
- conv_w: bfloat16 [9, 512, 4], replicated, may hold values from -0.09375 to 0.09375
- embed_w: bfloat16 [16, 1024], replicated, may hold values from -1.5 to 1.5
- mod_table: bfloat16 [1000, 2048], replicated, may hold values from -3 to 3
- qkv_w: bfloat16 [1024, 3072], replicated, may hold values from -0.1875 to 0.1875
- out_w: bfloat16 [1024, 1024], replicated, may hold values from -0.1875 to 0.1875
- proj_w: bfloat16 [1024, 768], replicated, may hold values from -0.1875 to 0.1875
- dino: bfloat16 [8, 1024, 768], P('img', 'slab'), may hold values from -6 to 6
Outputs:
- grad_feats: bfloat16 [8, 32, 128, 512], P('img', 'slab')
- grad_proj: float32 [1024, 768], replicated
- grad_conv: float32 [9, 512, 4], replicated
- loss: float32 [], replicated
All inputs are finite; a program needn't handle non-finite values.
Results may differ from a plain program's by a relative error of at most 0.024.
Values may be sent and summed in bfloat16 or wider, within the bound.
A program may use at most 128 MiB of HBM per device.

v0:
```python
import jax
import jax.numpy as jnp
from jax import lax
from jax.sharding import PartitionSpec as P

HEAD_DIM = 64
latent_scale = 0.18215
norm_eps = 1e-06
cosine_eps = 1e-06


def extended(cells, sides, width):
    for axis, dim in sides:
        count = lax.axis_size(axis)
        ends = count - 1
        head = lax.slice_in_dim(cells, 0, width, axis=dim)
        tail = lax.slice_in_dim(cells, cells.shape[dim] - width, cells.shape[dim], axis=dim)
        cells = jnp.concatenate(
            [
                lax.ppermute(tail, axis, [(i, (i + 1) % count) for i in range(ends)]),
                cells,
                lax.ppermute(head, axis, [((i + 1) % count, i) for i in range(ends)]),
            ],
            axis=dim,
        )
    return cells


def conv_out(padded, conv_w):
    rows = padded.shape[0] - 2
    cols = padded.shape[1] - 2
    total = jnp.zeros((rows * cols, conv_w.shape[2]), jnp.float32)
    for tap in range(9):
        view = padded[tap // 3 : tap // 3 + rows, tap % 3 : tap % 3 + cols]
        total = total + jnp.dot(
            view.reshape(rows * cols, -1), conv_w[tap], preferred_element_type=jnp.float32
        )
    return total.reshape(rows, cols, -1) * latent_scale


def contract_first(left, right):
    return lax.dot_general(
        left, right, (((0,), (0,)), ((), ())), preferred_element_type=jnp.float32
    )


def contract_last(left, right):
    return lax.dot_general(
        left, right, (((1,), (1,)), ((), ())), preferred_element_type=jnp.float32
    )


def conv_back(padded, grad_pad, conv_w):
    rows = grad_pad.shape[0] - 2
    cols = grad_pad.shape[1] - 2
    center = grad_pad[1:-1, 1:-1].reshape(rows * cols, -1)
    grad_in = jnp.zeros((rows * cols, conv_w.shape[1]), jnp.float32)
    parts = []
    for tap in range(9):
        row_off = tap // 3
        col_off = tap % 3
        g_view = grad_pad[
            2 - row_off : 2 - row_off + rows, 2 - col_off : 2 - col_off + cols
        ].reshape(rows * cols, -1)
        grad_in = grad_in + contract_last(g_view, conv_w[tap])
        f_view = padded[row_off : row_off + rows, col_off : col_off + cols].reshape(rows * cols, -1)
        parts.append(contract_first(f_view, center))
    return (grad_in.reshape(rows, cols, -1), jnp.stack(parts, 0))


def patchify(latent):
    rows, cols, chans = latent.shape
    blocks = latent.reshape(rows // 2, 2, cols // 2, 2, chans).transpose(0, 2, 1, 3, 4)
    return blocks.reshape(rows // 2 * (cols // 2), 4 * chans)


def unpatchify(tokens, rows, cols):
    chans = tokens.shape[1] // 4
    blocks = tokens.reshape(rows // 2, cols // 2, 2, 2, chans).transpose(0, 2, 1, 3, 4)
    return blocks.reshape(rows, cols, chans)


def cosine_grad(projected, target):
    norm_p = jnp.sqrt(jnp.sum(projected * projected, -1, keepdims=True) + cosine_eps)
    norm_t = jnp.sqrt(jnp.sum(target * target, -1, keepdims=True) + cosine_eps)
    cosine = jnp.sum(projected * target, -1, keepdims=True) / (norm_p * norm_t)
    grad = cosine * projected / (norm_p * norm_p) - target / (norm_p * norm_t)
    return (cosine[:, 0], grad)


def local(feats, labels, conv_w, embed_w, mod_table, qkv_w, out_w, proj_w, dino):
    image = feats[0]
    rows, cols, chans = image.shape
    width = qkv_w.shape[0]
    heads = width // HEAD_DIM
    scale = HEAD_DIM ** (-0.5)
    rimmed = extended(image, (("slab", 0),), 1)
    padded = jnp.pad(rimmed, ((0, 0), (1, 1), (0, 0)))
    tokens = patchify(conv_out(padded, conv_w))
    count = tokens.shape[0]
    embed_f = embed_w.astype(jnp.float32)
    start = jnp.dot(tokens, embed_f, precision=lax.Precision.HIGHEST)
    row = lax.dynamic_index_in_dim(mod_table, labels[0], 0, keepdims=False).astype(jnp.float32)
    mean = jnp.mean(start, -1, keepdims=True)
    cent = start - mean
    inv = lax.rsqrt(jnp.mean(cent * cent, -1, keepdims=True) + norm_eps)
    normed = cent * inv
    modded = (normed * (1.0 + row[width:]) + row[:width]).astype(jnp.bfloat16)
    qkv = jnp.dot(modded, qkv_w, preferred_element_type=jnp.float32).astype(jnp.bfloat16)
    query = qkv[:, :width]
    key = qkv[:, width : 2 * width]
    value = qkv[:, 2 * width :]
    key_all, value_all = (
        lax.all_gather(key, "slab", axis=0, tiled=True),
        lax.all_gather(value, "slab", axis=0, tiled=True),
    )
    q3 = query.reshape(count, heads, HEAD_DIM)
    k3 = key_all.reshape(-1, heads, HEAD_DIM)
    v3 = value_all.reshape(-1, heads, HEAD_DIM)
    scores = jnp.einsum("qhd,khd->hqk", q3, k3, preferred_element_type=jnp.float32) * scale
    top = jnp.max(scores, -1, keepdims=True)
    expo = jnp.exp(scores - top)
    total = jnp.sum(expo, -1)
    attended = (
        jnp.einsum(
            "hqk,khd->qhd", expo.astype(jnp.bfloat16), v3, preferred_element_type=jnp.float32
        )
        / total.T[:, :, None]
    )
    attended = attended.reshape(count, width).astype(jnp.bfloat16)
    lse = top[..., 0] + jnp.log(total)
    resid = start + jnp.dot(attended, out_w, preferred_element_type=jnp.float32)
    resid_b = resid.astype(jnp.bfloat16)
    projected = jnp.dot(resid_b, proj_w, preferred_element_type=jnp.float32)
    cosine, grad_p = cosine_grad(projected, dino[0].astype(jnp.float32))
    grad_pb = grad_p.astype(jnp.bfloat16)
    proj_part = contract_first(resid_b, grad_pb)
    grad_resid = contract_last(grad_pb, proj_w)
    grad_att = contract_last(grad_resid.astype(jnp.bfloat16), out_w).astype(jnp.bfloat16)
    g3 = grad_att.reshape(count, heads, HEAD_DIM)
    delta = jnp.sum(
        g3.astype(jnp.float32) * attended.reshape(count, heads, HEAD_DIM).astype(jnp.float32), -1
    ).T
    probs = jnp.exp(scores - lse[..., None])
    dprobs = jnp.einsum("qhd,khd->hqk", g3, v3, preferred_element_type=jnp.float32)
    dscores = (probs * (dprobs - delta[..., None])).astype(jnp.bfloat16)
    grad_query = scale * jnp.einsum(
        "hqk,khd->qhd", dscores, k3, preferred_element_type=jnp.float32
    ).reshape(count, width)
    key_terms = scale * jnp.einsum(
        "hqk,qhd->khd", dscores, q3, preferred_element_type=jnp.float32
    ).reshape(-1, width)
    value_terms = jnp.einsum(
        "hqk,qhd->khd", probs.astype(jnp.bfloat16), g3, preferred_element_type=jnp.float32
    ).reshape(-1, width)
    grad_key, grad_value = (
        lax.psum_scatter(
            key_terms.astype(jnp.bfloat16), "slab", scatter_dimension=0, tiled=True
        ).astype(jnp.float32),
        lax.psum_scatter(
            value_terms.astype(jnp.bfloat16), "slab", scatter_dimension=0, tiled=True
        ).astype(jnp.float32),
    )
    grad_qkv = jnp.concatenate([grad_query, grad_key, grad_value], 1).astype(jnp.bfloat16)
    grad_mod = contract_last(grad_qkv, qkv_w)
    grad_norm = grad_mod * (1.0 + row[width:])
    grad_start = grad_resid + inv * (
        grad_norm
        - jnp.mean(grad_norm, -1, keepdims=True)
        - normed * jnp.mean(grad_norm * normed, -1, keepdims=True)
    )
    grad_tokens = jnp.dot(grad_start, embed_f.T, precision=lax.Precision.HIGHEST)
    grad_latent = (unpatchify(grad_tokens, rows, cols) * latent_scale).astype(jnp.bfloat16)
    grad_rim = extended(grad_latent, (("slab", 0),), 1)
    grad_pad = jnp.pad(grad_rim, ((0, 0), (1, 1), (0, 0)))
    grad_image, conv_part = conv_back(padded, grad_pad, conv_w)
    loss_part = jnp.sum(1.0 - cosine)
    grad_proj, grad_conv, loss_sum = lax.psum((proj_part, conv_part, loss_part), ("slab", "img"))
    groups = lax.axis_size("slab") * lax.axis_size("img")
    return (
        grad_image.astype(jnp.bfloat16)[None],
        grad_proj,
        grad_conv,
        loss_sum / (groups * count),
    )


def solution(mesh):
    in_specs = (
        P("img", "slab", None, None),
        P("img"),
        P(),
        P(),
        P(),
        P(),
        P(),
        P(),
        P("img", "slab", None),
    )
    out_specs = (P("img", "slab", None, None), P(), P(), P())
    return jax.shard_map(local, mesh=mesh, in_specs=in_specs, out_specs=out_specs, check_vma=False)
```

profile of v0, /device:TPU:0, one launch (start us, length us, event | category | flops | bytes accessed | tf_op | source)
XLA Modules:
  0.0 356.8 jit_solution(18336326718904891435)
XLA Ops:
  8.4 2.4 collective-permute-start
  25.2 1.9 copy.46
  29.6 4.8 %convolution_convert_fusion = bf16[256,3072]{1,0:T(8,128)(2,1)S(1)} fusion(bf16[1024,3072]{1,0:T(8,128)(2,1)} %param.14, f32[256,1024]{1,0:T(8,128)S(1)} %get-tuple-element.33, f32[1024]{0:T(1024)} %bitcast.264, f32[1024]{0:T(1024)S(1)} %bitcast.262, f32[256]{0:T(256)S(1)} %add_rsqrt_fusion, f32[256]{0:T(256)S(1)} %broadcast_multiply_fusion.2), kind=kOutput, calls=%fused_computation.16 | convolution fusion | flops 1612709888 | bytes 8923136 | tf_op jit(solution)/shard_map/dot_general | solution.py:109
  36.4 2.0 copy.48
  38.5 24.5 %all-gather.5.cloned.1.call-done = bf16[1024,1024]{1,0:T(8,128)(2,1)} async-done(((bf16[256,1024]{1,0:T(8,128)(2,1)}), bf16[1024,1024]{1,0:T(8,128)(2,1)}) %all-gather.5.cloned.1.call-update) | async-done | bytes 2097168 | tf_op jit(solution)/shard_map/all_gather | solution.py:114
  63.0 4.0 %copy.49 = bf16[1024,1024]{0,1:T(8,128)(2,1)} copy(bf16[1024,1024]{1,0:T(8,128)(2,1)} %all-gather.5.cloned.1.call-done) | data formatting | bytes 4194304 | tf_op jit(solution)/shard_map/all_gather | solution.py:114
  66.9 4.2 %multiply_reduce_fusion = (f32[16,256]{1,0:T(8,128)S(1)}, f32[16,256,1024]{2,1,0:T(8,128)S(1)}) fusion(bf16[256,16,64]{0,2,1:T(8,128)(2,1)} %bitcast.234, bf16[1024,16,64]{0,2,1:T(8,128)(2,1)} %bitcast.226), kind=kOutput, calls=%fused_computation.6 | convolution fusion | flops 545255424 | bytes 19415040 | tf_op jit(solution)/shard_map/qhd,khd->hqk/dot_general | solution.py:120
  71.2 3.6 %fusion = f32[16,256]{1,0:T(8,128)S(1)} fusion(f32[16,256,1024]{2,1,0:T(8,128)S(1)} %get-tuple-element.35, f32[16,256]{1,0:T(8,128)S(1)} %get-tuple-element.34), kind=kLoop, calls=%fused_computation.3 | loop fusion | flops 12578816 | bytes 16809984 | tf_op jit(solution)/shard_map/reduce_sum | solution.py:123
  74.8 2.3 copy-done.2
  77.9 9.2 %all-gather.3.cloned.1.call-done = bf16[1024,1024]{1,0:T(8,128)(2,1)} async-done(((bf16[256,1024]{1,0:T(8,128)(2,1)}), bf16[1024,1024]{1,0:T(8,128)(2,1)}) %all-gather.3.cloned.1.call-update) | async-done | bytes 2097168 | tf_op jit(solution)/shard_map/all_gather | solution.py:115
  87.1 3.9 %copy.47 = bf16[1024,1024]{0,1:T(8,128)(2,1)} copy(bf16[1024,1024]{1,0:T(8,128)(2,1)} %all-gather.3.cloned.1.call-done) | data formatting | bytes 4194304 | tf_op jit(solution)/shard_map/all_gather | solution.py:115
  91.0 8.3 %divide_convert_fusion = bf16[256,16,64]{0,2,1:T(8,128)(2,1)S(1)} fusion(bf16[1024,16,64]{0,2,1:T(8,128)(2,1)} %bitcast.231, f32[16,256,1024]{2,1,0:T(8,128)} %copy-done.2, f32[16,256]{1,0:T(8,128)} %copy-done.25, f32[256,16]{0,1:T(8,128)} %bitcast.261), kind=kOutput, calls=%fused_computation.83 | convolution fusion | flops 549978112 | bytes 19431424 | tf_op jit(solution)/shard_map/hqk,khd->qhd/dot_general | solution.py:125
  109.0 9.4 %multiply_convert_fusion = bf16[16,256,1024]{2,1,0:T(8,128)(2,1)S(1)} fusion(f32[16,256,1024]{2,1,0:T(8,128)} %copy-done.2, bf16[256,16,64]{0,2,1:T(8,128)(2,1)S(1)} %bitcast.229, bf16[1024,16,64]{0,2,1:T(8,128)(2,1)} %bitcast.232, f32[16,256]{1,0:T(8,128)S(1)} %bitcast.260, f32[16,256]{1,0:T(8,128)S(1)} %log_add_fusion), kind=kOutput, calls=%fused_computation | convolution fusion | flops 557842432 | bytes 27820032 | tf_op jit(solution)/shard_map/qhd,khd->hqk/dot_general | solution.py:145
  118.5 3.4 multiply_convert_fusion.1
  122.4 9.8 %fusion.12 = bf16[16,64,1024]{2,1,0:T(8,128)(2,1)} fusion(bf16[256,16,64]{0,2,1:T(8,128)(2,1)S(1)} %bitcast.230, f32[16,256,1024]{2,1,0:T(8,128)} %copy-done.2, f32[16,256]{1,0:T(8,128)S(1)} %log_add_fusion), kind=kOutput, calls=%fused_computation.19 | convolution fusion | flops 550502400 | bytes 19415040 | tf_op jit(solution)/shard_map/hqk,qhd->khd/dot_general | solution.py:153
  132.3 39.7 %psum.23 = f32[]{:T(128)} all-reduce(f32[]{:T(128)} %get-tuple-element.11), channel_id=1, replica_groups=mesh['slab'=4,'img'=8] {'slab','img'}, use_global_device_ids=true, to_apply=%region_15.16 | all-reduce | flops 1 | bytes 8 | tf_op jit(solution)/shard_map/psum | solution.py:178
  172.7 3.5 fusion.166
  176.3 6.9 %fusion.33 = bf16[16,64,256]{2,1,0:T(8,128)(2,1)} fusion(bf16[1024,16,64]{0,2,1:T(8,128)(2,1)S(1)} %bitcast.227, bf16[16,256,1024]{2,1,0:T(8,128)(2,1)} %copy-done.3), kind=kOutput, calls=%fused_computation.37 | convolution fusion | flops 537395200 | bytes 11010048 | tf_op jit(solution)/shard_map/hqk,khd->qhd/dot_general | solution.py:147
  183.1 4.4 %reduce-scatter.5.cloned.1.call-done = bf16[256,1024]{0,1:T(8,128)(2,1)} async-done(((bf16[1024,1024]{0,1:T(8,128)(2,1)}), bf16[256,1024]{0,1:T(8,128)(2,1)}) %reduce-scatter.5.cloned.1.call-update) | async-done | bytes 524304 | tf_op jit(solution)/shard_map/reduce_scatter | solution.py:160
  187.5 5.7 %fusion.160 = (f32[256]{0:T(256)S(1)}, f32[256]{0:T(256)S(1)}, f32[256,1024]{1,0:T(8,128)S(1)}) fusion(f32[256]{0:T(256)S(1)} %add_rsqrt_fusion, f32[256,1024]{1,0:T(8,128)} %copy-done.7, f32[256]{0:T(256)S(1)} %broadcast_multiply_fusion.2, f32[1024]{0:T(1024)S(1)} %bitcast.263, bf16[1024,3072]{1,0:T(8,128)(2,1)} %param.14, ...), kind=kOutput, calls=%fused_computation.197 | convolution fusion | flops 1616903680 | bytes 9969664 | tf_op jit(solution)/shard_map/dot_general | solution.py:48
  199.0 3.3 collective-permute-start.2
  209.8 2.1 add_convert_fusion
  211.9 132.6 %all-reduce.5.cloned.1.call-done = (f32[1024,768]{1,0:T(8,128)}, f32[9,512,4]{1,2,0:T(4,128)}) async-done(((f32[1024,768]{1,0:T(8,128)}, f32[9,512,4]{1,2,0:T(4,128)}), (f32[1024,768]{1,0:T(8,128)}, f32[9,512,4]{1,2,0:T(4,128)})) %all-reduce.5.cloned.1.call-update) | async-done | bytes 3219472 | tf_op jit(solution)/shard_map/psum | solution.py:178
  344.6 3.9 %copy.88 = f32[1024,768]{1,0:T(8,128)} copy(f32[1024,768]{1,0:T(8,128)} %get-tuple-element.41) | data formatting | bytes 6291456
  (134 shorter events, 44.3 us)
Async XLA Ops:
  7.2 92.2 %copy-start = (bf16[1024,1024]{1,0:T(8,128)(2,1)S(1)}, bf16[1024,1024]{1,0:T(8,128)(2,1)}, u32[]{:S(2)}) copy-start(bf16[1024,1024]{1,0:T(8,128)(2,1)} %param.15) | copy-start | bytes 6291460
  7.2 55.8 %all-gather.5.cloned.1.call-start = ((), (), s32[]{:S(2)}) async-start(), calls=%async_computation.3 | async-start | bytes 2621440 | tf_op jit(solution)/shard_map/all_gather | solution.py:114
  8.4 7.3 %collective-permute-start = (bf16[1,128,512]{2,1,0:T(8,128)(2,1)S(1)}, bf16[1,128,512]{2,1,0:T(8,128)(2,1)S(1)}, u32[]{:S(2)}, u32[]{:S(2)}) collective-permute-start(bf16[1,128,512]{2,1,0:T(8,128)(2,1)S(1)} %get-tuple-element.25), channel_id=1, source_target_pairs={{0,8},{8,16},{16,24},{1,9},{9,17},{17,25},{2,10},{10,18},{18,26},{... | collective-permute-start | bytes 393224 | tf_op jit(solution)/shard_map/ppermute | solution.py:20
  10.8 5.3 %collective-permute-start.1 = (bf16[1,128,512]{2,1,0:T(8,128)(2,1)S(1)}, bf16[1,128,512]{2,1,0:T(8,128)(2,1)S(1)}, u32[]{:S(2)}, u32[]{:S(2)}) collective-permute-start(bf16[1,128,512]{2,1,0:T(8,128)(2,1)S(1)} %get-tuple-element.26), channel_id=1, source_target_pairs={{8,0},{16,8},{24,16},{9,1},{17,9},{25,17},{10,2},{18,10},{26,18},{... | collective-permute-start | bytes 393224 | tf_op jit(solution)/shard_map/ppermute | solution.py:22
  29.3 5.1 %copy-start.7 = (f32[256,1024]{1,0:T(8,128)}, f32[256,1024]{1,0:T(8,128)S(1)}, u32[]{:S(2)}) copy-start(f32[256,1024]{1,0:T(8,128)S(1)} %get-tuple-element.33) | copy-start | bytes 3145732
  35.6 51.5 %all-gather.3.cloned.1.call-start = ((), (), s32[]{:S(2)}) async-start(), calls=%async_computation.2 | async-start | bytes 2621440 | tf_op jit(solution)/shard_map/all_gather | solution.py:115
  36.4 146.7 %reduce-scatter.3.cloned.1.call-start = ((), (), s32[]{:S(2)}) async-start(), calls=%async_computation.4 | async-start | bytes 2621440 | tf_op jit(solution)/shard_map/reduce_scatter | solution.py:157
  71.1 6.0 %copy-start.2 = (f32[16,256,1024]{2,1,0:T(8,128)}, f32[16,256,1024]{2,1,0:T(8,128)S(1)}, u32[]{:S(2)}) copy-start(f32[16,256,1024]{2,1,0:T(8,128)S(1)} %get-tuple-element.35) | copy-start | bytes 50331652
  71.1 6.1 %copy-start.25 = (f32[16,256]{1,0:T(8,128)}, f32[16,256]{1,0:T(8,128)S(1)}, u32[]{:S(2)}) copy-start(f32[16,256]{1,0:T(8,128)S(1)} %get-tuple-element.34) | copy-start | bytes 49156
  91.0 8.3 %copy-start.8 = (f32[256,1024]{1,0:T(8,128)S(1)}, f32[256,1024]{1,0:T(8,128)}, u32[]{:S(2)}) copy-start(f32[256,1024]{1,0:T(8,128)} %copy-done.7) | copy-start | bytes 3145732
  99.4 1.6 copy-start.23
  109.0 9.5 %copy-start.13 = (bf16[256,1024]{0,1:T(8,128)(2,1)S(1)}, bf16[256,1024]{0,1:T(8,128)(2,1)}, u32[]{:S(2)}) copy-start(bf16[256,1024]{0,1:T(8,128)(2,1)} %copy.48) | copy-start | bytes 1572868
  118.5 3.9 %copy-start.3 = (bf16[16,256,1024]{2,1,0:T(8,128)(2,1)}, bf16[16,256,1024]{2,1,0:T(8,128)(2,1)S(1)}, u32[]{:S(2)}) copy-start(bf16[16,256,1024]{2,1,0:T(8,128)(2,1)S(1)} %multiply_convert_fusion) | copy-start | bytes 25165828
  122.4 65.1 %reduce-scatter.5.cloned.1.call-start = ((), (), s32[]{:S(2)}) async-start(), calls=%async_computation.5 | async-start | bytes 2621440 | tf_op jit(solution)/shard_map/reduce_scatter | solution.py:160
  132.3 44.0 %copy-start.6 = (bf16[1024,1024]{0,1:T(8,128)(2,1)S(1)}, bf16[1024,1024]{0,1:T(8,128)(2,1)}, u32[]{:S(2)}) copy-start(bf16[1024,1024]{0,1:T(8,128)(2,1)} %copy.49) | copy-start | bytes 6291460
  132.3 212.3 %all-reduce.5.cloned.1.call-start = ((), (), s32[]{:S(2)}) async-start(), calls=%async_computation.6 | async-start | bytes 6438912 | tf_op jit(solution)/shard_map/psum | solution.py:178
  187.5 5.7 %copy-start.9 = (f32[256,1024]{1,0:T(8,128)S(1)}, f32[256,1024]{1,0:T(8,128)}, u32[]{:S(2)}) copy-start(f32[256,1024]{1,0:T(8,128)} %copy-done.7) | copy-start | bytes 3145732
  187.5 5.7 %copy-start.11 = (f32[256,1024]{1,0:T(8,128)S(1)}, f32[256,1024]{1,0:T(8,128)}, u32[]{:S(2)}) copy-start(f32[256,1024]{1,0:T(8,128)} %copy-done.10) | copy-start | bytes 3145732
  187.5 5.7 %copy-start.26 = (bf16[16,1024]{1,0:T(8,128)(2,1)S(1)}, bf16[16,1024]{1,0:T(8,128)(2,1)}, u32[]{:S(2)}) copy-start(bf16[16,1024]{1,0:T(8,128)(2,1)} %param.12) | copy-start | bytes 98308
  197.4 6.7 %copy-start.20 = (bf16[1,128,512]{2,1,0:T(8,128)(2,1)S(1)}, bf16[1,128,512]{2,1,0:T(8,128)(2,1)}, u32[]{:S(2)}) copy-start(bf16[1,128,512]{2,1,0:T(8,128)(2,1)} %copy-done.18) | copy-start | bytes 393220
  197.6 7.7 %collective-permute-start.3 = (bf16[1,128,4]{2,1,0:T(8,128)(2,1)S(1)}, bf16[1,128,4]{2,1,0:T(8,128)(2,1)S(1)}, u32[]{:S(2)}, u32[]{:S(2)}) collective-permute-start(bf16[1,128,4]{2,1,0:T(8,128)(2,1)S(1)} %get-tuple-element.28), channel_id=1, source_target_pairs={{8,0},{16,8},{24,16},{9,1},{17,9},{25,17},{10,2},{18,10},{26,18},{... | collective-permute-start | bytes 3080 | tf_op jit(solution)/shard_map/ppermute | solution.py:22
  199.0 6.5 %collective-permute-start.2 = (bf16[1,128,4]{2,1,0:T(8,128)(2,1)S(1)}, bf16[1,128,4]{2,1,0:T(8,128)(2,1)S(1)}, u32[]{:S(2)}, u32[]{:S(2)}) collective-permute-start(bf16[1,128,4]{2,1,0:T(8,128)(2,1)S(1)} %get-tuple-element.27), channel_id=1, source_target_pairs={{0,8},{8,16},{16,24},{1,9},{9,17},{17,25},{2,10},{10,18},{18,26},{... | collective-permute-start | bytes 3080 | tf_op jit(solution)/shard_map/ppermute | solution.py:20
  344.6 4.6 %copy-start.1 = (bf16[1024,1024]{1,0:T(8,128)(2,1)S(1)}, bf16[1024,1024]{1,0:T(8,128)(2,1)}, u32[]{:S(2)}) copy-start(bf16[1024,1024]{1,0:T(8,128)(2,1)} %param.15) | copy-start | bytes 6291460
  344.6 3.9 %copy-start.28 = (f32[9,512,4]{1,2,0:T(4,128)S(1)}, f32[9,512,4]{1,2,0:T(4,128)}, u32[]{:S(2)}) copy-start(f32[9,512,4]{1,2,0:T(4,128)} %get-tuple-element.42) | copy-start | bytes 221188
  (15 other events, 16.8 us)
Sparse Core Ops, SparseCore 0:
  35.8 27.1 all-gather.4
  64.5 22.5 all-gather.2
  122.5 31.3 reduce-scatter.2
  156.3 31.1 reduce-scatter.4
  205.5 139.0 all-reduce.4
where the time goes:
time: 358 us; the launch traced here: 357 us
  waiting for transfers between devices  172 us (48%)
  matrix products  78.6 us (22%)
  blocking collectives  39.7 us (11%)
  local copies, waits for them, and re-layouts  32.2 us (9%)
  between operations  16.7 us (5%)
  other arithmetic  9.29 us (3%)
  starting transfers between devices  8.48 us (2%)
    psum x1, waiting for transfers between devices, local(): lax.psum((proj_part, conv_part, loss_part), ('slab', 'img'))  133 us
    psum x1, blocking collectives, local(): lax.psum((proj_part, conv_part, loss_part), ('slab', 'img'))  39.7 us
    all_gather x1, waiting for transfers between devices, local(): lax.all_gather(key, 'slab', axis=0, tiled=True)  24.5 us
    dot_general x12, matrix products, contract_last(): lax.dot_general(left, right, (((1,), (1,)), ((), ())), preferred_element_...  15.3 us
    unnamed x62, local copies, waits for them, and re-layouts  12.8 us
    dot_general x1, matrix products, local(): jnp.einsum('hqk,qhd->khd', probs.astype(jnp.bfloat16), g3, preferred_elem...  9.81 us
    dot_general x1, matrix products, local(): jnp.einsum('qhd,khd->hqk', g3, v3, preferred_element_type=jnp.float32)  9.44 us
    all_gather x1, waiting for transfers between devices, local(): lax.all_gather(value, 'slab', axis=0, tiled=True)  9.23 us
  transfers between devices with their start and end apart: 9, of which 5 were waited for; matrix products, arithmetic and copies ran while one was open for 13% of the time, Pallas kernels for 0%

commit v1 on v0

--- a/solution.py
+++ b/solution.py
@@ -175,7 +175,9 @@
     grad_pad = jnp.pad(grad_rim, ((0, 0), (1, 1), (0, 0)))
     grad_image, conv_part = conv_back(padded, grad_pad, conv_w)
     loss_part = jnp.sum(1.0 - cosine)
-    grad_proj, grad_conv, loss_sum = lax.psum((proj_part, conv_part, loss_part), ("slab", "img"))
+    grad_proj, grad_conv, loss_sum = lax.psum(
+        lax.psum((proj_part, conv_part, loss_part), "img"), "slab"
+    )
     groups = lax.axis_size("slab") * lax.axis_size("img")
     return (
         grad_image.astype(jnp.bfloat16)[None],

time: 358 us -> 415 us (1.16)
  waiting for transfers between devices: 172 us -> 234 us
  blocking collectives: 39.7 us -> 29.8 us
    reduce_scatter x1, waiting for transfers between devices: 4.35 us -> 33.6 us  [local(): lax.psum_scatter(value_terms.astype(jnp.bfloat16), 'slab', scatter_dimens...]
    psum x1 -> x2, waiting for transfers between devices: 133 us -> 154 us  [the longest x1 88.6 us: local(): lax.psum((proj_part, conv_part, loss_part), 'img')]
    reduce_scatter x1, waiting for transfers between devices: 0.01 us -> 10.9 us  [local(): lax.psum_scatter(key_terms.astype(jnp.bfloat16), 'slab', scatter_dimensio...]
    psum x1 -> x2, blocking collectives: 39.7 us -> 29.8 us  [the longest x1 23.1 us: local(): lax.psum((proj_part, conv_part, loss_part), 'img')]
    unnamed x62 -> x70, local copies, waits for them, and re-layouts: 12.8 us -> 13.9 us
  transfers between devices with their start and end apart: 9 -> 10, of which waited for: 5 -> 7; matrix products, arithmetic and copies ran while one was open for 13% -> 12% of each run, Pallas kernels for 0% -> 0%
where the time goes in v1:
time: 415 us; the launch traced here: 414 us
  waiting for transfers between devices  234 us (56%)
  matrix products  82.3 us (20%)
  local copies, waits for them, and re-layouts  33.3 us (8%)
  blocking collectives  29.8 us (7%)
  between operations  17 us (4%)
  other arithmetic  9.29 us (2%)
  starting transfers between devices  8.65 us (2%)
    psum x1, waiting for transfers between devices, local(): lax.psum((proj_part, conv_part, loss_part), 'img')  88.6 us
    psum x1, waiting for transfers between devices, local(): lax.psum(lax.psum((proj_part, conv_part, loss_part), 'img'), 'slab')  65.6 us
    reduce_scatter x1, waiting for transfers between devices, local(): lax.psum_scatter(value_terms.astype(jnp.bfloat16), 'slab', scatter_dimens...  33.6 us
    all_gather x1, waiting for transfers between devices, local(): lax.all_gather(key, 'slab', axis=0, tiled=True)  24.5 us
    psum x1, blocking collectives, local(): lax.psum((proj_part, conv_part, loss_part), 'img')  23.1 us
    dot_general x12, matrix products, contract_last(): lax.dot_general(left, right, (((1,), (1,)), ((), ())), preferred_element_...  19 us
    unnamed x70, local copies, waits for them, and re-layouts  13.9 us
    reduce_scatter x1, waiting for transfers between devices, local(): lax.psum_scatter(key_terms.astype(jnp.bfloat16), 'slab', scatter_dimensio...  10.9 us
  transfers between devices with their start and end apart: 10, of which 7 were waited for; matrix products, arithmetic and copies ran while one was open for 12% of the time, Pallas kernels for 0%

profile of v1, /device:TPU:0, one launch (start us, length us, event | category | flops | bytes accessed | tf_op | source)
XLA Modules:
  0.0 414.1 jit_solution(851235638440522062)
XLA Ops:
  8.4 2.4 collective-permute-start
  29.6 4.8 %convolution_convert_fusion = bf16[256,3072]{1,0:T(8,128)(2,1)S(1)} fusion(bf16[1024,3072]{1,0:T(8,128)(2,1)} %param.14, f32[256,1024]{1,0:T(8,128)S(1)} %get-tuple-element.35, f32[1024]{0:T(1024)} %bitcast.264, f32[1024]{0:T(1024)S(1)} %bitcast.262, f32[256]{0:T(256)S(1)} %add_rsqrt_fusion, f32[256]{0:T(256)S(1)} %broadcast_multiply_fusion.2), kind=kOutput, calls=%fused_computation.16 | convolution fusion | flops 1612709888 | bytes 8923136 | tf_op jit(solution)/shard_map/dot_general | solution.py:109
  38.5 24.5 %all-gather.5.cloned.1.call-done = bf16[1024,1024]{1,0:T(8,128)(2,1)} async-done(((bf16[256,1024]{1,0:T(8,128)(2,1)}), bf16[1024,1024]{1,0:T(8,128)(2,1)}) %all-gather.5.cloned.1.call-update) | async-done | bytes 2097168 | tf_op jit(solution)/shard_map/all_gather | solution.py:114
  62.9 4.0 copy.49
  66.9 4.2 %multiply_reduce_fusion = (f32[16,256]{1,0:T(8,128)S(1)}, f32[16,256,1024]{2,1,0:T(8,128)S(1)}) fusion(bf16[256,16,64]{0,2,1:T(8,128)(2,1)} %bitcast.234, bf16[1024,16,64]{0,2,1:T(8,128)(2,1)} %bitcast.226), kind=kOutput, calls=%fused_computation.6 | convolution fusion | flops 545255424 | bytes 19415040 | tf_op jit(solution)/shard_map/qhd,khd->hqk/dot_general | solution.py:120
  71.1 3.6 fusion
  74.8 2.3 copy-done.2
  77.9 9.2 %all-gather.3.cloned.1.call-done = bf16[1024,1024]{1,0:T(8,128)(2,1)} async-done(((bf16[256,1024]{1,0:T(8,128)(2,1)}), bf16[1024,1024]{1,0:T(8,128)(2,1)}) %all-gather.3.cloned.1.call-update) | async-done | bytes 2097168 | tf_op jit(solution)/shard_map/all_gather | solution.py:115
  87.1 3.9 copy.47
  91.0 8.3 %divide_convert_fusion = bf16[256,16,64]{0,2,1:T(8,128)(2,1)S(1)} fusion(bf16[1024,16,64]{0,2,1:T(8,128)(2,1)} %bitcast.231, f32[16,256,1024]{2,1,0:T(8,128)} %copy-done.2, f32[16,256]{1,0:T(8,128)} %copy-done.29, f32[256,16]{0,1:T(8,128)} %bitcast.261), kind=kOutput, calls=%fused_computation.83 | convolution fusion | flops 549978112 | bytes 19431424 | tf_op jit(solution)/shard_map/hqk,khd->qhd/dot_general | solution.py:125
  109.0 9.4 %multiply_convert_fusion = bf16[16,256,1024]{2,1,0:T(8,128)(2,1)S(1)} fusion(f32[16,256,1024]{2,1,0:T(8,128)} %copy-done.2, bf16[256,16,64]{0,2,1:T(8,128)(2,1)S(1)} %bitcast.229, bf16[1024,16,64]{0,2,1:T(8,128)(2,1)} %bitcast.232, f32[16,256]{1,0:T(8,128)S(1)} %bitcast.260, f32[16,256]{1,0:T(8,128)S(1)} %log_add_fusion), kind=kOutput, calls=%fused_computation | convolution fusion | flops 557842432 | bytes 27820032 | tf_op jit(solution)/shard_map/qhd,khd->hqk/dot_general | solution.py:145
  118.4 3.4 multiply_convert_fusion.1
  122.4 9.8 %fusion.12 = bf16[16,64,1024]{2,1,0:T(8,128)(2,1)} fusion(bf16[256,16,64]{0,2,1:T(8,128)(2,1)S(1)} %bitcast.230, f32[16,256,1024]{2,1,0:T(8,128)} %copy-done.2, f32[16,256]{1,0:T(8,128)S(1)} %log_add_fusion), kind=kOutput, calls=%fused_computation.19 | convolution fusion | flops 550502400 | bytes 19415040 | tf_op jit(solution)/shard_map/hqk,qhd->khd/dot_general | solution.py:153
  132.3 3.6 fusion.166
  135.9 6.9 %fusion.33 = bf16[16,64,256]{2,1,0:T(8,128)(2,1)} fusion(bf16[1024,16,64]{0,2,1:T(8,128)(2,1)S(1)} %bitcast.227, bf16[16,256,1024]{2,1,0:T(8,128)(2,1)} %copy-done.3), kind=kOutput, calls=%fused_computation.37 | convolution fusion | flops 537395200 | bytes 11010048 | tf_op jit(solution)/shard_map/hqk,khd->qhd/dot_general | solution.py:147
  142.7 10.9 %reduce-scatter.3.cloned.1.call-done = bf16[256,1024]{0,1:T(8,128)(2,1)} async-done(((bf16[1024,1024]{0,1:T(8,128)(2,1)}), bf16[256,1024]{0,1:T(8,128)(2,1)}) %reduce-scatter.3.cloned.1.call-update) | async-done | bytes 524304 | tf_op jit(solution)/shard_map/reduce_scatter | solution.py:157
  153.7 33.6 %reduce-scatter.5.cloned.1.call-done = bf16[256,1024]{0,1:T(8,128)(2,1)} async-done(((bf16[1024,1024]{0,1:T(8,128)(2,1)}), bf16[256,1024]{0,1:T(8,128)(2,1)}) %reduce-scatter.5.cloned.1.call-update) | async-done | bytes 524304 | tf_op jit(solution)/shard_map/reduce_scatter | solution.py:160
  187.3 5.7 %fusion.160 = (f32[256]{0:T(256)S(1)}, f32[256]{0:T(256)S(1)}, f32[256,1024]{1,0:T(8,128)S(1)}) fusion(f32[256]{0:T(256)S(1)} %add_rsqrt_fusion, f32[256,1024]{1,0:T(8,128)} %copy-done.7, f32[256]{0:T(256)S(1)} %broadcast_multiply_fusion.2, f32[1024]{0:T(1024)S(1)} %bitcast.263, bf16[1024,3072]{1,0:T(8,128)(2,1)} %param.14, ...), kind=kOutput, calls=%fused_computation.197 | convolution fusion | flops 1616903680 | bytes 9969664 | tf_op jit(solution)/shard_map/dot_general | solution.py:48
  199.1 23.1 %psum.46 = f32[]{:T(128)} all-reduce(f32[]{:T(128)} %get-tuple-element.13), channel_id=1, replica_groups=mesh['slab'=4,'img'=8] {'img'}, use_global_device_ids=true, to_apply=%region_17.18 | all-reduce | flops 1 | bytes 8 | tf_op jit(solution)/shard_map/psum | solution.py:179
  222.1 6.7 %psum.47 = f32[]{:T(128)} all-reduce(f32[]{:T(128)} %psum.46), channel_id=1, replica_groups=mesh['slab'=4,'img'=8] {'slab'}, use_global_device_ids=true, to_apply=%region_18.19 | all-reduce | flops 1 | bytes 8 | tf_op jit(solution)/shard_map/psum | solution.py:178
  231.0 3.3 collective-permute-start.2
  241.7 88.6 %all-reduce.7.cloned.1.call-done = (f32[1024,768]{1,0:T(8,128)}, f32[9,512,4]{1,2,0:T(4,128)}) async-done(((f32[1024,768]{1,0:T(8,128)}, f32[9,512,4]{1,2,0:T(4,128)}), (f32[1024,768]{1,0:T(8,128)}, f32[9,512,4]{1,2,0:T(4,128)})) %all-reduce.7.cloned.1.call-update) | async-done | bytes 3219472 | tf_op jit(solution)/shard_map/psum | solution.py:179
  335.9 65.6 %all-reduce.9.cloned.1.call-done = (f32[1024,768]{1,0:T(8,128)}, f32[9,512,4]{1,2,0:T(4,128)}) async-done(((f32[1024,768]{1,0:T(8,128)}, f32[9,512,4]{1,2,0:T(4,128)}), (f32[1024,768]{1,0:T(8,128)}, f32[9,512,4]{1,2,0:T(4,128)})) %all-reduce.9.cloned.1.call-update) | async-done | bytes 3219472 | tf_op jit(solution)/shard_map/psum | solution.py:178
  401.5 3.9 copy.90
  (146 shorter events, 55.3 us)
Async XLA Ops:
  7.2 92.2 %copy-start = (bf16[1024,1024]{1,0:T(8,128)(2,1)S(1)}, bf16[1024,1024]{1,0:T(8,128)(2,1)}, u32[]{:S(2)}) copy-start(bf16[1024,1024]{1,0:T(8,128)(2,1)} %param.15) | copy-start | bytes 6291460
  7.2 55.8 %all-gather.5.cloned.1.call-start = ((), (), s32[]{:S(2)}) async-start(), calls=%async_computation.3 | async-start | bytes 2621440 | tf_op jit(solution)/shard_map/all_gather | solution.py:114
  8.4 7.3 %collective-permute-start = (bf16[1,128,512]{2,1,0:T(8,128)(2,1)S(1)}, bf16[1,128,512]{2,1,0:T(8,128)(2,1)S(1)}, u32[]{:S(2)}, u32[]{:S(2)}) collective-permute-start(bf16[1,128,512]{2,1,0:T(8,128)(2,1)S(1)} %get-tuple-element.27), channel_id=1, source_target_pairs={{0,8},{8,16},{16,24},{1,9},{9,17},{17,25},{2,10},{10,18},{18,26},{... | collective-permute-start | bytes 393224 | tf_op jit(solution)/shard_map/ppermute | solution.py:20
  10.8 5.3 %collective-permute-start.1 = (bf16[1,128,512]{2,1,0:T(8,128)(2,1)S(1)}, bf16[1,128,512]{2,1,0:T(8,128)(2,1)S(1)}, u32[]{:S(2)}, u32[]{:S(2)}) collective-permute-start(bf16[1,128,512]{2,1,0:T(8,128)(2,1)S(1)} %get-tuple-element.28), channel_id=1, source_target_pairs={{8,0},{16,8},{24,16},{9,1},{17,9},{25,17},{10,2},{18,10},{26,18},{... | collective-permute-start | bytes 393224 | tf_op jit(solution)/shard_map/ppermute | solution.py:22
  29.3 5.1 %copy-start.7 = (f32[256,1024]{1,0:T(8,128)}, f32[256,1024]{1,0:T(8,128)S(1)}, u32[]{:S(2)}) copy-start(f32[256,1024]{1,0:T(8,128)S(1)} %get-tuple-element.35) | copy-start | bytes 3145732
  35.6 51.5 %all-gather.3.cloned.1.call-start = ((), (), s32[]{:S(2)}) async-start(), calls=%async_computation.2 | async-start | bytes 2621440 | tf_op jit(solution)/shard_map/all_gather | solution.py:115
  36.4 117.3 %reduce-scatter.3.cloned.1.call-start = ((), (), s32[]{:S(2)}) async-start(), calls=%async_computation.4 | async-start | bytes 2621440 | tf_op jit(solution)/shard_map/reduce_scatter | solution.py:157
  71.1 6.0 %copy-start.2 = (f32[16,256,1024]{2,1,0:T(8,128)}, f32[16,256,1024]{2,1,0:T(8,128)S(1)}, u32[]{:S(2)}) copy-start(f32[16,256,1024]{2,1,0:T(8,128)S(1)} %get-tuple-element.37) | copy-start | bytes 50331652
  71.1 6.1 %copy-start.29 = (f32[16,256]{1,0:T(8,128)}, f32[16,256]{1,0:T(8,128)S(1)}, u32[]{:S(2)}) copy-start(f32[16,256]{1,0:T(8,128)S(1)} %get-tuple-element.36) | copy-start | bytes 49156
  91.0 8.3 %copy-start.8 = (f32[256,1024]{1,0:T(8,128)S(1)}, f32[256,1024]{1,0:T(8,128)}, u32[]{:S(2)}) copy-start(f32[256,1024]{1,0:T(8,128)} %copy-done.7) | copy-start | bytes 3145732
  109.0 9.5 %copy-start.15 = (bf16[256,1024]{0,1:T(8,128)(2,1)S(1)}, bf16[256,1024]{0,1:T(8,128)(2,1)}, u32[]{:S(2)}) copy-start(bf16[256,1024]{0,1:T(8,128)(2,1)} %copy.48) | copy-start | bytes 1572868
  118.4 3.9 copy-start.3
  122.3 64.9 %reduce-scatter.5.cloned.1.call-start = ((), (), s32[]{:S(2)}) async-start(), calls=%async_computation.5 | async-start | bytes 2621440 | tf_op jit(solution)/shard_map/reduce_scatter | solution.py:160
  132.2 198.0 %all-reduce.7.cloned.1.call-start = ((), (), s32[]{:S(2)}) async-start(), calls=%async_computation.6 | async-start | bytes 6438912 | tf_op jit(solution)/shard_map/psum | solution.py:179
  187.3 5.7 %copy-start.9 = (f32[256,1024]{1,0:T(8,128)S(1)}, f32[256,1024]{1,0:T(8,128)}, u32[]{:S(2)}) copy-start(f32[256,1024]{1,0:T(8,128)} %copy-done.7) | copy-start | bytes 3145732
  187.3 5.7 %copy-start.11 = (f32[256,1024]{1,0:T(8,128)S(1)}, f32[256,1024]{1,0:T(8,128)}, u32[]{:S(2)}) copy-start(f32[256,1024]{1,0:T(8,128)} %copy-done.10) | copy-start | bytes 3145732
  187.3 5.7 %copy-start.30 = (bf16[16,1024]{1,0:T(8,128)(2,1)S(1)}, bf16[16,1024]{1,0:T(8,128)(2,1)}, u32[]{:S(2)}) copy-start(bf16[16,1024]{1,0:T(8,128)(2,1)} %param.12) | copy-start | bytes 98308
  194.3 35.2 %copy-start.16 = (bf16[4,64,2,2,4]{4,3,1,2,0:T(2,128)(2,1)}, bf16[4,64,2,2,4]{4,3,1,2,0:T(2,128)(2,1)S(1)}, u32[]{:S(2)}) copy-start(bf16[4,64,2,2,4]{4,3,1,2,0:T(2,128)(2,1)S(1)} %copy.51) | copy-start | bytes 24580
  199.0 202.5 %all-reduce.9.cloned.1.call-start = ((), (), s32[]{:S(2)}) async-start(), calls=%async_computation.7 | async-start | bytes 6438912 | tf_op jit(solution)/shard_map/psum | solution.py:178
  229.5 6.1 %copy-start.17 = (bf16[4,64,2,2,4]{4,3,1,2,0:T(2,128)(2,1)S(1)}, bf16[4,64,2,2,4]{4,3,1,2,0:T(2,128)(2,1)}, u32[]{:S(2)}) copy-start(bf16[4,64,2,2,4]{4,3,1,2,0:T(2,128)(2,1)} %copy-done.16) | copy-start | bytes 24580
  229.5 6.2 %collective-permute-start.3 = (bf16[1,128,4]{2,1,0:T(8,128)(2,1)S(1)}, bf16[1,128,4]{2,1,0:T(8,128)(2,1)S(1)}, u32[]{:S(2)}, u32[]{:S(2)}) collective-permute-start(bf16[1,128,4]{2,1,0:T(8,128)(2,1)S(1)} %get-tuple-element.30), channel_id=1, source_target_pairs={{8,0},{16,8},{24,16},{9,1},{17,9},{25,17},{10,2},{18,10},{26,18},{... | collective-permute-start | bytes 3080 | tf_op jit(solution)/shard_map/ppermute | solution.py:22
  231.0 4.9 %collective-permute-start.2 = (bf16[1,128,4]{2,1,0:T(8,128)(2,1)S(1)}, bf16[1,128,4]{2,1,0:T(8,128)(2,1)S(1)}, u32[]{:S(2)}, u32[]{:S(2)}) collective-permute-start(bf16[1,128,4]{2,1,0:T(8,128)(2,1)S(1)} %get-tuple-element.29), channel_id=1, source_target_pairs={{0,8},{8,16},{16,24},{1,9},{9,17},{17,25},{2,10},{10,18},{18,26},{... | collective-permute-start | bytes 3080 | tf_op jit(solution)/shard_map/ppermute | solution.py:20
  401.5 4.6 %copy-start.1 = (bf16[1024,1024]{1,0:T(8,128)(2,1)S(1)}, bf16[1024,1024]{1,0:T(8,128)(2,1)}, u32[]{:S(2)}) copy-start(bf16[1024,1024]{1,0:T(8,128)(2,1)} %param.15) | copy-start | bytes 6291460
  401.5 3.9 copy-start.32
  (20 other events, 27.2 us)
Sparse Core Ops, SparseCore 0:
  35.7 27.1 all-gather.4
  64.5 22.5 all-gather.2
  122.5 31.1 reduce-scatter.2
  156.1 31.1 reduce-scatter.4
  199.1 131.1 all-reduce.6
  332.6 68.9 all-reduce.8
